TPU v7x, 256 devices: a whole 4x4x8 slice. The times are simulated.
256 devices in a mesh: rows: 64 (over x, z_hi, y, core), feat: 4 (over z_lo).
Axes of the slice: x: 4, y: 4, z: 8 (z_hi: 2, z_lo: 4; z = z_hi * 4 + z_lo), core: 2. Of those that a mesh axis runs over, the one named last changes fastest.
Arguments:
- bins: int32 [65536, 512], P('rows', 'feat'), may hold values from -2147483648 to 2147483647, as said below
- hessian: float32 [262144], P('rows'), may hold values from 0.05 to 1
- thresholds: float32 [128], replicated, may hold values from 0.02 to 0.98
Outputs:
- cuts: float32 [512, 128], P('feat')
Inputs may be any that keep to these rules, and one draw needn't show every extreme that they name: `bins`: each word holds the bin ids, 0 to 255, of rows 4i to 4i + 3 of one feature, row 4i + k in bits 8k to 8k + 7 of the two's complement word.
All inputs are finite; a program needn't handle non-finite values.
Results may differ from a plain program's by a relative error of at most 0.000065.
Values sent between devices are 32-bit elements; how exact they have to be, the bound alone decides.
A program may use at most 192 MiB of HBM per device.

v0:
```python
import math

import jax
import jax.numpy as jnp
from jax import lax
from jax.sharding import PartitionSpec as P

BINS = 256


def split_up(x, dim, devices):
    before, after = (x.shape[:dim], x.shape[dim + 1 :])
    return jnp.moveaxis(x.reshape(*before, devices, -1, *after), dim, 0)


def sent_and_summed(x, axis, dim):
    devices = lax.axis_size(axis)
    pieces = lax.all_to_all(split_up(x, dim, devices), axis, 0, 0, tiled=True)
    return jnp.sum(pieces, axis=0)


def joined_along(pieces, dim):
    pieces = jnp.moveaxis(pieces, 0, dim)
    lengths = pieces.shape
    return pieces.reshape(*lengths[:dim], lengths[dim] * lengths[dim + 1], *lengths[dim + 2 :])


def from_everyone(x, axis):
    copies = jnp.broadcast_to(x, (lax.axis_size(axis), *x.shape))
    return lax.all_to_all(copies, axis, split_axis=0, concat_axis=0, tiled=True)


def gather_directly(x, axis, dim):
    return joined_along(from_everyone(x, axis), dim)


def unpack(words):
    parts = [jnp.bitwise_and(jnp.right_shift(words, 8 * k), 255) for k in range(4)]
    stacked = jnp.stack(parts, axis=1)
    return stacked.reshape(words.shape[0] * 4, words.shape[1])


def histogram(columns, weights):
    count, width = columns.shape
    limit = max(8, 1048576 // (width * 16))
    block = math.gcd(count, limit)
    col_blocks = columns.reshape(count // block, block, width)
    wt_blocks = weights.reshape(count // block, block)
    levels = jnp.arange(16, dtype=jnp.int32)

    def add_block(total, item):
        col_part, wt_part = item
        high = jnp.right_shift(col_part, 4)
        low = jnp.bitwise_and(col_part, 15)
        high_hot = jnp.where(high[:, :, None] == levels, wt_part[:, None, None], 0.0)
        low_hot = (low[:, :, None] == levels).astype(jnp.float32)
        joint = jnp.einsum("rkh,rkl->khl", high_hot, low_hot, precision=lax.Precision.HIGHEST)
        return (total + joint, None)

    start = jnp.zeros((width, 16, 16), jnp.float32)
    total, unused = lax.scan(add_block, start, (col_blocks, wt_blocks))
    return total.reshape(width, BINS)


def cut_positions(hist, thresholds):
    cum = jnp.cumsum(hist, axis=1)
    before = cum - hist
    total = cum[:, -1]
    target = thresholds[None, :, None] * total[:, None, None]
    ratio = (target - before[:, None, :]) / (hist[:, None, :] + 1.0)
    return jnp.sum(jnp.clip(ratio, 0.0, 1.0), axis=2)


def local(bins, hessian, thresholds):
    local_ids = unpack(bins)
    hist = sent_and_summed(histogram(local_ids, hessian), "rows", 0)
    cuts = cut_positions(hist, thresholds)
    return gather_directly(cuts, "rows", 0)


def solution(mesh):
    in_specs = (P("rows", "feat"), P("rows"), P())
    out_specs = P("feat", None)
    return jax.shard_map(local, mesh=mesh, in_specs=in_specs, out_specs=out_specs, check_vma=False)
```

profile of v0, /device:TPU:1, one launch (start us, length us, event | category | flops | bytes accessed | tf_op | source)
XLA Modules:
  0.0 95.3 jit_solution(14017348286414728610)
XLA Ops:
  0.0 1.2 %and_bitcast_fusion.4 = (s32[1024,1,128]{2,0,1:T(8,128)S(1)}, s32[1024,1,128]{2,0,1:T(8,128)S(1)}, s32[1024,1,128]{2,0,1:T(8,128)S(1)}, s32[1024,1,128]{2,0,1:T(8,128)S(1)}) fusion(s32[1024,128]{1,0:T(8,128)} %param.5), kind=kLoop, calls=%fused_computation.19 | loop fusion | flops 1048576 | bytes 2621440 | tf_op jit(solution)/shard_map/stack | solution.py:39
  1.2 0.1 pad_add_fusion
  1.3 0.0 copy-start
  1.3 1.4 %copy.8 = s32[1024,4,128]{2,1,0:T(4,128)S(1)} copy(s32[1024,4,128]{2,0,1:T(8,128)S(1)} %pad_add_fusion) | data formatting | bytes 4194304 | tf_op jit(solution)/shard_map/stack | solution.py:39
  2.7 0.0 copy-done
  2.7 0.0 copy-start.1
  2.7 43.9 %while.12 = (s32[]{:T(128)}, f32[128,16,16]{2,1,0:T(8,128)}, s32[8,512,128]{2,1,0:T(8,128)S(1)}, f32[8,512]{1,0:T(8,128)S(1)}, s32[]{:T(128)}, /*index=5*/s32[]{:T(128)}) while((s32[]{:T(128)}, f32[128,16,16]{2,1,0:T(8,128)}, s32[8,512,128]{2,1,0:T(8,128)S(1)}, f32[8,512]{1,0:T(8,128)S(1)}, s32[]{:T(128)}, ...), condition=%wide.region_1.2_spmd.clone.clone, body=%wide.region_0.1_spmd.clone.clone.sunk | while | flops 204668928 | bytes 2627671 | solution.py:61
  2.8 0.1 copy.19
  2.9 0.1 shift-right-arithmetic_bitcast_fusion.2
  3.0 4.2 %fusion.16 = f32[128,16,16]{2,1,0:T(8,128)} fusion(s32[512,128]{0,1:T(8,128)S(1)} %get-tuple-element.118, f32[512]{0:T(512)S(1)} %bitcast.30, s32[512,128]{0,1:T(8,128)S(1)} %get-tuple-element.119, f32[128,16,16]{2,1,0:T(8,128)} %get-tuple-element.127, pred[]{:T(512)S(6)} %compare.3), kind=kOutput, calls=%fused_computation.9.clone.1 | convolution fusion | flops 204537856 | bytes 788481 | tf_op jit(solution)/shard_map/while/body/eval_jaxpr/rkh,rkl->khl/dot_general | solution.py:57
  7.2 0.1 copy.19
  7.3 0.1 shift-right-arithmetic_bitcast_fusion.2
  7.4 5.4 %fusion.16 = f32[128,16,16]{2,1,0:T(8,128)} fusion(s32[512,128]{0,1:T(8,128)S(1)} %get-tuple-element.118, f32[512]{0:T(512)S(1)} %bitcast.30, s32[512,128]{0,1:T(8,128)S(1)} %get-tuple-element.119, f32[128,16,16]{2,1,0:T(8,128)} %get-tuple-element.127, pred[]{:T(512)S(6)} %compare.3), kind=kOutput, calls=%fused_computation.9.clone.1 | convolution fusion | flops 204537856 | bytes 788481 | tf_op jit(solution)/shard_map/while/body/eval_jaxpr/rkh,rkl->khl/dot_general | solution.py:57
  12.8 0.1 copy.19
  13.0 0.1 shift-right-arithmetic_bitcast_fusion.2
  13.1 5.4 %fusion.16 = f32[128,16,16]{2,1,0:T(8,128)} fusion(s32[512,128]{0,1:T(8,128)S(1)} %get-tuple-element.118, f32[512]{0:T(512)S(1)} %bitcast.30, s32[512,128]{0,1:T(8,128)S(1)} %get-tuple-element.119, f32[128,16,16]{2,1,0:T(8,128)} %get-tuple-element.127, pred[]{:T(512)S(6)} %compare.3), kind=kOutput, calls=%fused_computation.9.clone.1 | convolution fusion | flops 204537856 | bytes 788481 | tf_op jit(solution)/shard_map/while/body/eval_jaxpr/rkh,rkl->khl/dot_general | solution.py:57
  18.5 0.1 copy.19
  18.6 0.1 shift-right-arithmetic_bitcast_fusion.2
  18.7 5.4 %fusion.16 = f32[128,16,16]{2,1,0:T(8,128)} fusion(s32[512,128]{0,1:T(8,128)S(1)} %get-tuple-element.118, f32[512]{0:T(512)S(1)} %bitcast.30, s32[512,128]{0,1:T(8,128)S(1)} %get-tuple-element.119, f32[128,16,16]{2,1,0:T(8,128)} %get-tuple-element.127, pred[]{:T(512)S(6)} %compare.3), kind=kOutput, calls=%fused_computation.9.clone.1 | convolution fusion | flops 204537856 | bytes 788481 | tf_op jit(solution)/shard_map/while/body/eval_jaxpr/rkh,rkl->khl/dot_general | solution.py:57
  24.1 0.1 copy.19
  24.3 0.1 shift-right-arithmetic_bitcast_fusion.2
  24.4 5.4 %fusion.16 = f32[128,16,16]{2,1,0:T(8,128)} fusion(s32[512,128]{0,1:T(8,128)S(1)} %get-tuple-element.118, f32[512]{0:T(512)S(1)} %bitcast.30, s32[512,128]{0,1:T(8,128)S(1)} %get-tuple-element.119, f32[128,16,16]{2,1,0:T(8,128)} %get-tuple-element.127, pred[]{:T(512)S(6)} %compare.3), kind=kOutput, calls=%fused_computation.9.clone.1 | convolution fusion | flops 204537856 | bytes 788481 | tf_op jit(solution)/shard_map/while/body/eval_jaxpr/rkh,rkl->khl/dot_general | solution.py:57
  29.8 0.1 copy.19
  29.9 0.1 shift-right-arithmetic_bitcast_fusion.2
  30.0 5.4 %fusion.16 = f32[128,16,16]{2,1,0:T(8,128)} fusion(s32[512,128]{0,1:T(8,128)S(1)} %get-tuple-element.118, f32[512]{0:T(512)S(1)} %bitcast.30, s32[512,128]{0,1:T(8,128)S(1)} %get-tuple-element.119, f32[128,16,16]{2,1,0:T(8,128)} %get-tuple-element.127, pred[]{:T(512)S(6)} %compare.3), kind=kOutput, calls=%fused_computation.9.clone.1 | convolution fusion | flops 204537856 | bytes 788481 | tf_op jit(solution)/shard_map/while/body/eval_jaxpr/rkh,rkl->khl/dot_general | solution.py:57
  35.4 0.1 copy.19
  35.6 0.1 shift-right-arithmetic_bitcast_fusion.2
  35.6 5.4 %fusion.16 = f32[128,16,16]{2,1,0:T(8,128)} fusion(s32[512,128]{0,1:T(8,128)S(1)} %get-tuple-element.118, f32[512]{0:T(512)S(1)} %bitcast.30, s32[512,128]{0,1:T(8,128)S(1)} %get-tuple-element.119, f32[128,16,16]{2,1,0:T(8,128)} %get-tuple-element.127, pred[]{:T(512)S(6)} %compare.3), kind=kOutput, calls=%fused_computation.9.clone.1 | convolution fusion | flops 204537856 | bytes 788481 | tf_op jit(solution)/shard_map/while/body/eval_jaxpr/rkh,rkl->khl/dot_general | solution.py:57
  41.1 0.1 copy.19
  41.2 0.1 shift-right-arithmetic_bitcast_fusion.2
  41.3 5.4 %fusion.16 = f32[128,16,16]{2,1,0:T(8,128)} fusion(s32[512,128]{0,1:T(8,128)S(1)} %get-tuple-element.118, f32[512]{0:T(512)S(1)} %bitcast.30, s32[512,128]{0,1:T(8,128)S(1)} %get-tuple-element.119, f32[128,16,16]{2,1,0:T(8,128)} %get-tuple-element.127, pred[]{:T(512)S(6)} %compare.3), kind=kOutput, calls=%fused_computation.9.clone.1 | convolution fusion | flops 204537856 | bytes 788481 | tf_op jit(solution)/shard_map/while/body/eval_jaxpr/rkh,rkl->khl/dot_general | solution.py:57
  46.7 1.7 %reshape_reshape.7 = f32[64,2,256]{2,1,0:T(2,128)S(1)} reshape(f32[128,16,16]{2,1,0:T(8,128)} %get-tuple-element.35) | data formatting | bytes 262144 | tf_op jit(solution)/shard_map/reshape;reshape | solution.py:13
  48.4 27.9 %all_to_all.10 = f32[64,2,256]{2,1,0:T(2,128)S(1)} all-to-all(f32[64,2,256]{2,1,0:T(2,128)S(1)} %reshape_reshape.7), channel_id=1, replica_groups=mesh['rows'=64,'feat'=4] {'rows'}, dimensions={0} | all-to-all | bytes 262144 | tf_op jit(solution)/shard_map/all_to_all | solution.py:18
  76.3 0.1 reduce_sum.18
  76.4 0.6 reduce-window.6
  77.0 0.2 slice_reduce_fusion
  77.2 0.2 reduce-window.9
  77.3 0.1 add_bitcast_fusion
  77.4 0.1 slice.16
  77.5 0.1 copy.12
  77.6 0.0 copy-done.1
  77.6 0.1 broadcast_multiply_fusion
  77.7 0.2 clamp_reduce_fusion
  77.9 16.8 %all_to_all.11 = f32[64,2,128]{2,1,0:T(2,128)S(1)} all-to-all(f32[64,2,128]{2,1,0:T(2,128)S(1)} %broadcast_in_dim.29), channel_id=1, replica_groups=mesh['rows'=64,'feat'=4] {'rows'}, dimensions={0} | all-to-all | bytes 131072 | tf_op jit(solution)/shard_map/all_to_all | solution.py:30
  94.7 0.6 copy.27
  (22 shorter events, 0.3 us)
Async XLA Ops:
  1.3 1.4 %copy-start = (f32[4096]{0:T(1024)S(1)}, f32[4096]{0:T(1024)}, u32[]{:S(2)}) copy-start(f32[4096]{0:T(1024)} %param.6) | copy-start | bytes 49156
  2.7 74.9 %copy-start.1 = (f32[128]{0:T(128)S(1)}, f32[128]{0:T(128)}, u32[]{:S(2)}) copy-start(f32[128]{0:T(128)} %param.7) | copy-start | bytes 1540
where the time goes:
time: 95.8 us; the launch traced here: 95.3 us
  blocking collectives  44.7 us (47%)
  matrix products  42 us (44%)
  local copies, waits for them, and re-layouts  5.36 us (6%)
  other arithmetic  2.98 us (3%)
    dot_general x8, matrix products, add_block(): jnp.einsum('rkh,rkl->khl', high_hot, low_hot, precision=lax.Precision.HIG...  42 us
    all_to_all x1, blocking collectives, sent_and_summed(): pieces = lax.all_to_all(split_up(x, dim, devices), axis, 0, 0, tiled=True)  27.9 us
    all_to_all x1, blocking collectives, from_everyone(): return lax.all_to_all(copies, axis, split_axis=0, concat_axis=0, tiled=True)  16.8 us

commit v1 on v0

v1 whole, which is shorter than its diff:
```python
import functools

import jax
import jax.numpy as jnp
import numpy as np
from jax import lax
from jax.experimental import pallas as pl
from jax.experimental.pallas import tpu as pltpu
from jax.sharding import PartitionSpec as P

OFFSETS = sorted(
    ((dx, dy) for dx in range(4) for dy in range(4)),
    key=lambda o: -(min(o[0], 4 - o[0]) + min(o[1], 4 - o[1])),
)
BARRIER_STEP = 3


def row_of(x, z, y, core):
    return ((x * 2 + z) * 4 + y) * 2 + core


def digit_patterns():
    r = lax.broadcasted_iota(jnp.int32, (16, 128), 0)
    low = [[((r + 16 * p) << (8 * b)).astype(jnp.int16) for p in range(2)] for b in range(2)]
    high = [((r % 8) << (5 + 8 * b)).astype(jnp.int16) for b in range(2)]
    return low, high


def spread_weights(h_ref, pieces_ref):
    lane = lax.broadcasted_iota(jnp.int32, (8, 128), 1)
    parts = [h_ref[pl.ds(s, 8, stride=4), :] for s in range(4)]
    for k in range(4):
        index = (lane % 32) * 4 + k
        rows = jnp.zeros((8, 128), jnp.float32)
        for s in range(4):
            rows = jnp.where(lane // 32 == s, jnp.take_along_axis(parts[s], index, axis=1), rows)
        lead = rows.astype(jnp.bfloat16).astype(jnp.float32)
        rest = rows - lead
        for c in range(8):
            both = [jnp.broadcast_to(v[c : c + 1], (8, 128)) for v in (lead, rest)]
            pieces_ref[c, k] = jnp.concatenate(both, axis=0).astype(jnp.bfloat16)


def group_histogram(words_ref, pieces_ref, g, low, high):
    words = words_ref.at[pl.ds(pl.multiple_of(g * 8, 8), 8)]
    one = jnp.ones((16, 128), jnp.bfloat16)
    zero = jnp.zeros((16, 128), jnp.bfloat16)
    acc = jnp.zeros((128, 256), jnp.float32)
    for c in range(8):
        pieces = [pieces_ref[c, k] for k in range(4)]
        lhs_rows, rhs_rows = [], []
        for j in range(8):
            w = jnp.broadcast_to(words[pl.ds(j, 1), pl.ds(128 * c, 128)], (16, 128))
            halves = [w.astype(jnp.int16), (w >> 16).astype(jnp.int16)]
            lhs_cols, rhs_cols = [], []
            for k in range(4):
                b = k % 2
                l = halves[k // 2] & jnp.int16(31 << (8 * b))
                h = halves[k // 2] & jnp.int16(np.array(224 << (8 * b), np.uint16).astype(np.int16))
                lhs_cols.append(jnp.where(h == high[b], pieces[k], zero))
                rhs_cols.append(jnp.concatenate([jnp.where(l == low[b][p], one, zero) for p in range(2)], axis=0))
            lhs_rows.append(jnp.concatenate(lhs_cols, axis=1))
            rhs_rows.append(jnp.concatenate(rhs_cols, axis=1))
        lhs = jnp.concatenate(lhs_rows, axis=0)
        rhs = jnp.concatenate(rhs_rows, axis=0).astype(jnp.float8_e4m3fn)
        acc = acc + lax.dot_general(lhs, rhs, (((1,), (1,)), ((), ())), preferred_element_type=jnp.float32)
    block = lax.broadcasted_iota(jnp.int32, (8, 256), 1) // 32
    out = jnp.zeros((8, 256), jnp.float32)
    for j in range(8):
        out = out + jnp.where(block == j, acc[16 * j : 16 * j + 8] + acc[16 * j + 8 : 16 * j + 16], 0.0)
    return out


def three_pieces(v):
    a = v.astype(jnp.bfloat16)
    v = v - a.astype(jnp.float32)
    b = v.astype(jnp.bfloat16)
    v = v - b.astype(jnp.float32)
    return [a, b, v.astype(jnp.bfloat16)]


def cut_positions(hist, thresholds):
    sub = lax.broadcasted_iota(jnp.int32, (8, 256), 0)
    block = lax.broadcasted_iota(jnp.int32, (8, 256), 1) // 32
    upto = hist
    for shift in (1, 2, 4):
        upto = upto + jnp.where(sub >= shift, pltpu.roll(upto, shift, 0), 0.0)
    above = jnp.where(sub >= 1, pltpu.roll(upto, 1, 0), 0.0)

    def diagonal(v):
        rows = jnp.concatenate([jnp.where(block == f, v, 0.0) for f in range(8)], axis=0)
        return jnp.concatenate(three_pieces(rows), axis=1)

    rhs = jnp.concatenate([diagonal(hist), diagonal(above)], axis=1)
    l_out = lax.broadcasted_iota(jnp.int32, (32, 256), 0)
    l_in = lax.broadcasted_iota(jnp.int32, (32, 256), 1) % 32
    earlier = (l_in < l_out).astype(jnp.float32).astype(jnp.bfloat16)
    same = (l_in == l_out).astype(jnp.float32).astype(jnp.bfloat16)
    ones = jnp.ones((32, 256), jnp.bfloat16)
    lhs = jnp.concatenate(
        [
            jnp.concatenate([earlier] * 3 + [ones] * 3, axis=1),
            jnp.concatenate([same] * 3 + [jnp.zeros_like(ones)] * 3, axis=1),
        ],
        axis=0,
    )
    out = lax.dot_general(lhs, rhs, (((1,), (1,)), ((), ())), preferred_element_type=jnp.float32)
    before, own = out[:32], out[32:]
    scale = 1.0 / (own + 1.0)
    last = before[31:32] + own[31:32]
    rows = []
    for f in range(8):
        target = thresholds * last[:, 8 * f + 7 : 8 * f + 8]
        part = jnp.zeros((32, 128), jnp.float32)
        for h in range(8):
            col = 8 * f + h
            ratio = (target - before[:, col : col + 1]) * scale[:, col : col + 1]
            part = part + jnp.clip(ratio, 0.0, 1.0)
        rows.append(jnp.sum(part, axis=0, keepdims=True))
    return jnp.concatenate(rows, axis=0)


def kernel(
    bins_ref, h_ref, t_ref, o_ref,
    raw, words, pieces, sent, got, swap_out, swap_in, own_cuts, cuts,
    load_sem, send_sem, recv_sem, swap_send, swap_recv, cut_send, cut_recv,
):
    r = lax.axis_index("rows")
    feat = lax.axis_index("feat")
    core = r % 2
    y = (r // 2) % 4
    z = (r // 8) % 2
    x = r // 16
    chip = x * 4 + y

    def device(dx, dy, c):
        return (row_of((x + dx) % 4, z, (y + dy) % 4, c), feat)

    partner = (row_of(x, 1 - z, y, 1), feat)
    mesh_ids = dict(device_id_type=pl.DeviceIdType.MESH)

    loads = [
        pltpu.make_async_copy(bins_ref.at[pl.ds(128 * c, 128)], raw.at[pl.ds(128 * c, 128)], load_sem.at[c])
        for c in range(8)
    ]
    for load in loads:
        load.start()

    barrier = pltpu.get_barrier_semaphore()
    for dx, dy in OFFSETS[:-1]:
        pl.semaphore_signal(barrier, inc=1, device_id=device(dx, dy, 1), **mesh_ids)

    @pl.when(core == 0)
    def _():
        pl.semaphore_signal(barrier, inc=1, device_id=device(0, 0, 1), **mesh_ids)

    @pl.when(core == 1)
    def _():
        for dx, dy in OFFSETS:
            pl.semaphore_signal(barrier, inc=1, device_id=device(dx, dy, 0), **mesh_ids)
        pl.semaphore_signal(barrier, inc=1, device_id=partner, **mesh_ids)

    low, high = digit_patterns()
    spread_weights(h_ref, pieces)
    for c in range(8):
        loads[c].wait()
        words[:, pl.ds(128 * c, 128)] = raw[pl.ds(128 * c, 128), :].T

    def send(s):
        dx, dy = OFFSETS[s]
        return pltpu.make_async_remote_copy(
            src_ref=sent.at[s], dst_ref=got.at[2 * chip + core], send_sem=send_sem, recv_sem=recv_sem,
            device_id=device(dx, dy, 1), **mesh_ids,
        )

    for s in range(15):
        dx, dy = OFFSETS[s]
        g = ((x + dx) % 4) * 4 + (y + dy) % 4
        sent[s] = group_histogram(words, pieces, g, low, high)
        if s == BARRIER_STEP:

            @pl.when(core == 0)
            def _():
                pl.semaphore_wait(barrier, 16)

            @pl.when(core == 1)
            def _():
                pl.semaphore_wait(barrier, 32)

            for e in range(s):
                send(e).start()
        if s >= BARRIER_STEP:
            send(s).start()

    sent[15] = group_histogram(words, pieces, chip, low, high)

    @pl.when(core == 0)
    def _():
        send(15).start()

    def cut_copy(dx, dy, c):
        return pltpu.make_async_remote_copy(
            src_ref=own_cuts, dst_ref=cuts.at[chip], send_sem=cut_send, recv_sem=cut_recv,
            device_id=device(dx, dy, c), **mesh_ids,
        )

    def wait_all(ref, count, sem):
        part = ref.at[pl.ds(0, count)]
        pltpu.make_async_copy(part, part, sem).wait()

    @pl.when(core == 1)
    def _():
        got[2 * chip + 1] = sent[15]
        wait_all(got, 31, recv_sem)
        sums = [got[i] for i in range(32)]
        while len(sums) > 1:
            sums = [a + b for a, b in zip(sums[::2], sums[1::2])]
        swap_out[...] = sums[0]
        swap = pltpu.make_async_remote_copy(
            src_ref=swap_out, dst_ref=swap_in, send_sem=swap_send, recv_sem=swap_recv,
            device_id=partner, **mesh_ids,
        )
        swap.start()
        swap.wait()
        mine = cut_positions(sums[0] + swap_in[...], t_ref[...])
        own_cuts[...] = mine
        for dx, dy in OFFSETS[:-1]:
            for c in range(2):
                cut_copy(dx, dy, c).start()
        cut_copy(0, 0, 0).start()
        cuts[chip] = mine
        wait_all(cuts, 15, cut_recv)
        wait_all(sent, 15, send_sem)

    @pl.when(core == 0)
    def _():
        wait_all(cuts, 16, cut_recv)
        wait_all(sent, 16, send_sem)

    o_ref[...] = cuts[pl.ds(0, 16)].reshape(128, 128)

    @pl.when(core == 1)
    def _():
        wait_all(cuts, 31, cut_send)


def sketch(bins, hessian, thresholds):
    return pl.pallas_call(
        kernel,
        out_shape=jax.ShapeDtypeStruct((128, 128), jnp.float32),
        in_specs=[
            pl.BlockSpec(memory_space=pl.ANY),
            pl.BlockSpec(memory_space=pltpu.VMEM),
            pl.BlockSpec(memory_space=pltpu.VMEM),
        ],
        out_specs=pl.BlockSpec(memory_space=pltpu.VMEM),
        scratch_shapes=[
            pltpu.VMEM((1024, 128), jnp.int32),
            pltpu.VMEM((128, 1024), jnp.int32),
            pltpu.VMEM((8, 4, 16, 128), jnp.bfloat16),
            pltpu.VMEM((16, 8, 256), jnp.float32),
            pltpu.VMEM((32, 8, 256), jnp.float32),
            pltpu.VMEM((8, 256), jnp.float32),
            pltpu.VMEM((8, 256), jnp.float32),
            pltpu.VMEM((8, 128), jnp.float32),
            pltpu.VMEM((31, 8, 128), jnp.float32),
            pltpu.SemaphoreType.DMA((8,)),
            pltpu.SemaphoreType.DMA,
            pltpu.SemaphoreType.DMA,
            pltpu.SemaphoreType.DMA,
            pltpu.SemaphoreType.DMA,
            pltpu.SemaphoreType.DMA,
            pltpu.SemaphoreType.DMA,
        ],
        compiler_params=pltpu.CompilerParams(collective_id=0, has_side_effects=True),
        name="sketch",
    )(bins, hessian.reshape(32, 128), thresholds.reshape(1, 128))


def solution(mesh):
    in_specs = (P("rows", "feat"), P("rows"), P())
    out_specs = P("feat", None)
    return jax.shard_map(sketch, mesh=mesh, in_specs=in_specs, out_specs=out_specs, check_vma=False)
```

time: 95.8 us -> 33.1 us (0.35)
  blocking collectives: 44.7 us -> 0 us
  matrix products: 42 us -> 0 us
  Pallas kernels: 0 us -> 31.4 us
  local copies, waits for them, and re-layouts: 5.36 us -> 1.47 us
  other arithmetic: 2.98 us -> 0 us
    all_to_all x2 -> x0, blocking collectives: 44.7 us -> none  [the longest x1 27.9 us: sent_and_summed(): pieces = lax.all_to_all(split_up(x, dim, devices), axis, 0, 0, tiled=True)]
    dot_general x8 -> x0, matrix products: 42 us -> none  [add_block(): jnp.einsum('rkh,rkl->khl', high_hot, low_hot, precision=lax.Precision.HIG...]
    pallas_call x0 -> x1, Pallas kernels: none -> 31.4 us  [sketch(): pl.pallas_call(kernel, out_shape=jax.ShapeDtypeStruct((128, 128), jnp.flo...]
    another operation x2 -> x0, local copies, waits for them, and re-layouts: 3.08 us -> none  [the longest x1 1.73 us: split_up(): return jnp.moveaxis(x.reshape(*before, devices, -1, *after), dim, 0)]
    another operation x4 -> x0, other arithmetic: 2.1 us -> none  [the longest x2 1.32 us: unpack(): stacked = jnp.stack(parts, axis=1)]
    dynamic_slice x24 -> x0, local copies, waits for them, and re-layouts: 1.26 us -> none  [histogram(): total, unused = lax.scan(add_block, start, (col_blocks, wt_blocks))]
where the time goes in v1:
time: 33.1 us; the launch traced here: 32.9 us
  Pallas kernels  31.4 us (95%)
  local copies, waits for them, and re-layouts  1.47 us (4%)
    pallas_call x1, Pallas kernels, sketch(): pl.pallas_call(kernel, out_shape=jax.ShapeDtypeStruct((128, 128), jnp.flo...  31.4 us
    unnamed x1, local copies, waits for them, and re-layouts  1.47 us

profile of v1, /device:TPU:1, one launch (start us, length us, event | category | flops | bytes accessed | tf_op | source)
XLA Modules:
  0.0 32.9 jit_solution(13851923194405769090)
XLA Ops:
  0.0 31.4 %sketch.1 = f32[128,128]{1,0:T(8,128)} custom-call(s32[1024,128]{1,0:T(8,128)} %bins_ref.1, f32[32,128]{1,0:T(8,128)} %bitcast.2, f32[1,128]{1,0:T(1,128)} %bitcast.3), custom_call_target="tpu_custom_call" | custom-call | tf_op jit(solution)/shard_map/sketch/pallas_call | solution.py:248
  31.4 1.5 %copy.5 = f32[128,128]{1,0:T(8,128)} copy(f32[128,128]{1,0:T(8,128)} %sketch.1) | data formatting | bytes 131072

commit v2 on v1

v2 whole, which is shorter than its diff:
```python
import functools

import jax
import jax.numpy as jnp
import numpy as np
from jax import lax
from jax.experimental import pallas as pl
from jax.experimental.pallas import tpu as pltpu
from jax.sharding import PartitionSpec as P

OFFSETS = sorted(
    ((dx, dy) for dx in range(4) for dy in range(4)),
    key=lambda o: -(min(o[0], 4 - o[0]) + min(o[1], 4 - o[1])),
)
X_ORDER = (2, 1, 3, 0)
BARRIER_STEP = 7
BATCHES = {7: ((0, 0, 4), (1, 0, 4)), 9: ((2, 0, 2),), 11: ((2, 2, 2),)}
FINISH_AT = 3
F8 = jnp.float8_e4m3fn


def row_of(x, z, y, core):
    return ((x * 2 + z) * 4 + y) * 2 + core


def digit_patterns():
    r = lax.broadcasted_iota(jnp.int32, (32, 128), 0)
    low = [(r << (8 * b)).astype(jnp.int16) for b in range(2)]
    high = [((r[:16] % 8) << (5 + 8 * b)).astype(jnp.int16) for b in range(2)]
    return low, high


def spread_weights(h_ref, pieces_ref):
    lane = lax.broadcasted_iota(jnp.int32, (8, 128), 1)
    parts = [h_ref[pl.ds(s, 8, stride=4), :] for s in range(4)]
    for k in range(4):
        index = (lane % 32) * 4 + k
        rows = jnp.zeros((8, 128), jnp.float32)
        for s in range(4):
            rows = jnp.where(lane // 32 == s, jnp.take_along_axis(parts[s], index, axis=1), rows)
        lead = rows.astype(jnp.bfloat16).astype(jnp.float32)
        rest = rows - lead
        for c in range(8):
            both = [jnp.broadcast_to(v[c : c + 1], (8, 128)) for v in (lead, rest)]
            pieces_ref[c, k] = jnp.concatenate(both, axis=0).astype(jnp.bfloat16)


def group_chunk(words_ref, pieces_ref, g, c, low, high, accs):
    words = words_ref.at[pl.ds(pl.multiple_of(g * 8, 8), 8)]
    zero = jnp.zeros((16, 128), jnp.bfloat16)
    one8 = jnp.ones((32, 128), F8)
    zero8 = jnp.zeros((32, 128), F8)
    halves = []
    for j in range(8):
        w = jnp.broadcast_to(words[pl.ds(j, 1), pl.ds(128 * c, 128)], (16, 128))
        halves.append([w.astype(jnp.int16), (w >> 16).astype(jnp.int16)])
    for q in range(2):
        lhs_rows, rhs_rows = [], []
        for j in range(8):
            lhs_cols, rhs_cols = [], []
            for b in range(2):
                l = halves[j][q] & jnp.int16(31 << (8 * b))
                h = halves[j][q] & jnp.int16(np.array(224 << (8 * b), np.uint16).astype(np.int16))
                lhs_cols.append(jnp.where(h == high[b], pieces_ref[c, 2 * q + b], zero))
                rhs_cols.append(jnp.where(jnp.concatenate([l, l], axis=0) == low[b], one8, zero8))
            lhs_rows.append(jnp.concatenate(lhs_cols, axis=1))
            rhs_rows.append(jnp.concatenate(rhs_cols, axis=1))
        pltpu.matmul_push_rhs(jnp.concatenate(rhs_rows, axis=0), staging_register=c % 2, mxu_index=q, transpose=True)
        pltpu.matmul_acc_lhs(accs[q], jnp.concatenate(lhs_rows, axis=0), load_staged_rhs=c % 2)


def group_result(accs):
    a, b = (pltpu.matmul_pop(acc) for acc in accs)
    block = lax.broadcasted_iota(jnp.int32, (8, 256), 1) // 32
    out = None
    for j in range(8):
        lead, rest = slice(16 * j, 16 * j + 8), slice(16 * j + 8, 16 * j + 16)
        own = (a[lead] + b[lead]) + (a[rest] + b[rest])
        out = own if j == 0 else jnp.where(block == j, own, out)
    return out


def three_pieces(v):
    a = v.astype(jnp.bfloat16)
    v = v - a.astype(jnp.float32)
    b = v.astype(jnp.bfloat16)
    v = v - b.astype(jnp.float32)
    return [a, b, v.astype(jnp.bfloat16)]


def prefix_matrix():
    l_out = lax.broadcasted_iota(jnp.int32, (32, 256), 0)
    l_in = lax.broadcasted_iota(jnp.int32, (32, 256), 1) % 32
    both = jnp.concatenate([l_in < l_out, l_in == l_out], axis=0)
    return both.astype(jnp.float32).astype(jnp.bfloat16)


def cut_positions(hist, thresholds, prefix, accs):
    sub = lax.broadcasted_iota(jnp.int32, (8, 256), 0)
    block = lax.broadcasted_iota(jnp.int32, (8, 256), 1) // 32
    upto = hist
    for shift in (1, 2, 4):
        upto = upto + jnp.where(sub >= shift, pltpu.roll(upto, shift, 0), 0.0)
    above = jnp.where(sub >= 1, pltpu.roll(upto, 1, 0), 0.0)

    def times_diagonal(q, lhs, v):
        rows = jnp.concatenate([jnp.where(block == f, v, 0.0) for f in range(8)], axis=0)
        rhs = jnp.concatenate([*three_pieces(rows), jnp.zeros((64, 256), jnp.bfloat16)], axis=0)
        pltpu.matmul_push_rhs(rhs, staging_register=0, mxu_index=q, transpose=True)
        pltpu.matmul_acc_lhs(accs[q], lhs, load_staged_rhs=0)

    def joined(v):
        return (v[:, :128] + pltpu.roll(v[:, :128], 64, 1)) + v[:, 128:]

    times_diagonal(0, prefix, hist)
    times_diagonal(1, jnp.ones((16, 256), jnp.bfloat16), above)
    out = joined(pltpu.matmul_pop(accs[0]))
    out_above = joined(pltpu.matmul_pop(accs[1])[:8])
    before = out[:32] + jnp.concatenate([out_above] * 4, axis=0)
    own = out[32:]
    scale = 1.0 / (own + 1.0)
    last = before[31:32] + own[31:32]
    rows = []
    for f in range(8):
        target = thresholds * last[:, 8 * f + 7 : 8 * f + 8]
        part = jnp.zeros((32, 128), jnp.float32)
        for h in range(8):
            col = 8 * f + h
            ratio = (target - before[:, col : col + 1]) * scale[:, col : col + 1]
            part = part + jnp.clip(ratio, 0.0, 1.0)
        rows.append(jnp.sum(part, axis=0, keepdims=True))
    return jnp.concatenate(rows, axis=0)


def body(
    accs,
    bins_ref, h_hbm, t_hbm, o_ref,
    h_ref, t_ref, raw, words, pieces, prefix, sent, got, part_out, part_in, own_cuts, cuts,
    load_sem, send_sem, recv_sem, part_send, part_recv, cut_send, cut_recv, ready,
):
    r = lax.axis_index("rows")
    feat = lax.axis_index("feat")
    core = r % 2
    y = (r // 2) % 4
    z = (r // 8) % 2
    x = r // 16
    chip = x * 4 + y
    mesh_ids = dict(device_id_type=pl.DeviceIdType.MESH)

    def device(dx, dy, c, dz=0):
        return (row_of((x + dx) % 4, (z + dz) % 2, (y + dy) % 4, c), feat)

    weights_load = pltpu.make_async_copy(h_hbm, h_ref, load_sem.at[8])
    thresholds_load = pltpu.make_async_copy(t_hbm, t_ref, load_sem.at[9])
    loads = [
        pltpu.make_async_copy(bins_ref.at[pl.ds(128 * c, 128)], raw.at[pl.ds(128 * c, 128)], load_sem.at[c])
        for c in range(8)
    ]
    weights_load.start()
    for load in loads:
        load.start()
    thresholds_load.start()

    barrier = pltpu.get_barrier_semaphore()
    for dx in X_ORDER[:3]:
        pl.semaphore_signal(barrier, inc=1, device_id=device(dx, 0, 1), **mesh_ids)

    @pl.when(core == 0)
    def _():
        pl.semaphore_signal(barrier, inc=1, device_id=device(0, 0, 1), **mesh_ids)

    @pl.when(core == 1)
    def _():
        for dz in (1, 0):
            for dy in X_ORDER:
                if dy or dz:
                    pl.semaphore_signal(barrier, inc=1, device_id=device(0, dy, 0, dz), **mesh_ids)

    low, high = digit_patterns()
    prefix[...] = prefix_matrix()
    weights_load.wait()
    spread_weights(h_ref, pieces)
    for c in range(8):
        loads[c].wait()
        words[:, pl.ds(128 * c, 128)] = raw[pl.ds(128 * c, 128), :].T
    thresholds_load.wait()

    def send(place, first, count):
        return pltpu.make_async_remote_copy(
            src_ref=sent.at[place, pl.ds(first, count)],
            dst_ref=got.at[2 * x + core, pl.ds(first, count)],
            send_sem=send_sem, recv_sem=recv_sem, device_id=device(X_ORDER[place], 0, 1), **mesh_ids,
        )

    def finish(s, accs):
        sent[s // 4, s % 4] = group_result(accs)
        if s == BARRIER_STEP:

            @pl.when(core == 1)
            def _():
                pl.semaphore_wait(barrier, 7)
                pl.semaphore_signal(ready, inc=1, device_id=device(0, 0, 0), **mesh_ids)

            @pl.when(core == 0)
            def _():
                pl.semaphore_wait(ready, 1)

        for batch in BATCHES.get(s, ()):
            send(*batch).start()

    pairs, cut_accs = (accs[:2], accs[2:4]), accs[4:]
    for acc in accs:
        pltpu.matmul_pop(acc)
    for s in range(16):
        g = ((x + X_ORDER[s // 4]) % 4) * 4 + s % 4
        for c in range(8):
            group_chunk(words, pieces, g, c, low, high, pairs[s % 2])
            if c + 1 == FINISH_AT and s:
                finish(s - 1, pairs[(s - 1) % 2])
    finish(15, pairs[1])

    def part_copy(dy, dz):
        return pltpu.make_async_remote_copy(
            src_ref=part_out.at[(y + dy) % 4], dst_ref=part_in.at[4 * z + y],
            send_sem=part_send, recv_sem=part_recv, device_id=device(0, dy, 1, dz), **mesh_ids,
        )

    def cut_copy(dx, dy, c):
        return pltpu.make_async_remote_copy(
            src_ref=own_cuts, dst_ref=cuts.at[chip], send_sem=cut_send, recv_sem=cut_recv,
            device_id=device(dx, dy, c), **mesh_ids,
        )

    def wait_all(ref, count, sem):
        whole = ref.at[pl.ds(0, count)]
        pltpu.make_async_copy(whole, whole, sem).wait()

    def tree_sum(terms):
        while len(terms) > 1:
            terms = [a + b for a, b in zip(terms[::2], terms[1::2])]
        return terms[0]

    @pl.when(core == 0)
    def _():
        send(3, 0, 4).start()
        pl.semaphore_wait(barrier, 7)
        pl.semaphore_signal(ready, inc=1, device_id=device(0, 0, 1), **mesh_ids)
        wait_all(cuts, 16, cut_recv)
        wait_all(sent, 4, send_sem)

    @pl.when(core == 1)
    def _():
        got[2 * x + 1] = sent[3]
        wait_all(got, 7, recv_sem)
        pl.semaphore_wait(ready, 1)
        for yy in range(4):
            part_out[yy] = tree_sum([got[i, yy] for i in range(8)])
        for dz in (1, 0):
            for dy in X_ORDER:
                if dy or dz:
                    part_copy(dy, dz).start()
        part_in[4 * z + y] = part_out[y]
        wait_all(part_in, 7, part_recv)
        hist = tree_sum([part_in[i] for i in range(8)])
        mine = cut_positions(hist, t_ref[...], prefix[...], cut_accs)
        own_cuts[...] = mine
        for dx, dy in OFFSETS[:-1]:
            for c in range(2):
                cut_copy(dx, dy, c).start()
        cut_copy(0, 0, 0).start()
        cuts[chip] = mine
        wait_all(sent, 3, send_sem)
        wait_all(part_in, 7, part_send)
        wait_all(cuts, 15, cut_recv)
        wait_all(cuts, 31, cut_send)

    o_ref[...] = cuts[pl.ds(0, 16)].reshape(128, 128)


def kernel(*refs):
    group = [pltpu.ACC(q)((128, 256), jnp.float32) for q in range(2)]
    cut = [pltpu.ACC(0)((64, 256), jnp.float32), pltpu.ACC(1)((16, 256), jnp.float32)]
    pl.run_scoped(lambda *accs: body(accs, *refs), *group, *group, *cut)


def sketch(bins, hessian, thresholds):
    dma = pltpu.SemaphoreType.DMA
    f32 = jnp.float32
    return pl.pallas_call(
        kernel,
        out_shape=pltpu.VMEM((128, 128), f32),
        in_specs=[pl.BlockSpec(memory_space=pl.ANY)] * 3,
        out_specs=pl.BlockSpec(memory_space=pltpu.VMEM),
        scratch_shapes=[
            pltpu.VMEM((32, 128), f32),
            pltpu.VMEM((1, 128), f32),
            pltpu.VMEM((1024, 128), jnp.int32),
            pltpu.VMEM((128, 1024), jnp.int32),
            pltpu.VMEM((8, 4, 16, 128), jnp.bfloat16),
            pltpu.VMEM((64, 256), jnp.bfloat16),
            pltpu.VMEM((4, 4, 8, 256), f32),
            pltpu.VMEM((8, 4, 8, 256), f32),
            pltpu.VMEM((4, 8, 256), f32),
            pltpu.VMEM((8, 8, 256), f32),
            pltpu.VMEM((8, 128), f32),
            pltpu.VMEM((31, 8, 128), f32),
            dma((10,)),
            dma, dma, dma, dma, dma, dma,
            pltpu.SemaphoreType.REGULAR,
        ],
        compiler_params=pltpu.CompilerParams(collective_id=0, has_side_effects=True),
        name="sketch",
    )(bins, hessian.reshape(32, 128), thresholds.reshape(1, 128))


def solution(mesh):
    in_specs = (P("rows", "feat"), P("rows"), P())
    out_specs = P("feat", None)
    return jax.shard_map(sketch, mesh=mesh, in_specs=in_specs, out_specs=out_specs, check_vma=False)
```

time: 33.1 us -> 26.6 us (0.80)
  Pallas kernels: 31.4 us -> 25.8 us
  local copies, waits for them, and re-layouts: 1.47 us -> 0.63 us
    pallas_call x1, Pallas kernels: 31.4 us -> 25.8 us  [sketch(): pl.pallas_call(kernel, out_shape=pltpu.VMEM((128, 128), f32), in_specs=[p...]
    unnamed x1, local copies, waits for them, and re-layouts: 1.47 us -> 0.63 us
where the time goes in v2:
time: 26.6 us; the launch traced here: 26.5 us
  Pallas kernels  25.8 us (97%)
  local copies, waits for them, and re-layouts  0.63 us (2%)
    pallas_call x1, Pallas kernels, sketch(): pl.pallas_call(kernel, out_shape=pltpu.VMEM((128, 128), f32), in_specs=[p...  25.8 us
    unnamed x1, local copies, waits for them, and re-layouts  0.63 us

profile of v2, /device:TPU:1, one launch (start us, length us, event | category | flops | bytes accessed | tf_op | source)
XLA Modules:
  0.0 26.5 jit_solution(5279978077329645816)
XLA Ops:
  0.0 25.8 %sketch.1 = f32[128,128]{1,0:T(8,128)S(1)} custom-call(s32[1024,128]{1,0:T(8,128)} %refs_0_.1, f32[32,128]{1,0:T(8,128)} %bitcast.2, f32[1,128]{1,0:T(1,128)} %bitcast.3), custom_call_target="tpu_custom_call" | custom-call | tf_op jit(solution)/shard_map/sketch/pallas_call | solution.py:289
  25.8 0.6 %copy.5 = f32[128,128]{1,0:T(8,128)} copy(f32[128,128]{1,0:T(8,128)S(1)} %sketch.1) | data formatting | bytes 131072
